TPU v7x, 32 devices: a whole 2x2x4 slice. The times are simulated.
32 devices in a mesh: row: 8 (over y, x, core), col: 4 (over z).
Axes of the slice: x: 2, y: 2, z: 4, core: 2. Of those that a mesh axis runs over, the one named last changes fastest.
Arguments:
- record: float32 [2, 32768], P(None, ('row', 'col')), may hold values from -5 to 5
Outputs:
- spectrum: float32 [256, 256, 2, 2, 256], P('row', 'col')
All inputs are finite; a program needn't handle non-finite values.
Results may differ from a plain program's by a relative error of at most 0.00011.
Values sent between devices are 32-bit elements; how exact they have to be, the bound alone decides.
No kernel may reach another device: no remote copies, remote signals or barrier semaphores. Data moves between devices by JAX's collectives and lax.ppermute only.
A program may use at most 64 MiB of HBM per device.

v0:
```python
import math
import jax
import jax.numpy as jnp
from jax import lax
from jax.sharding import PartitionSpec as P

C = 256
P_SIZE = 256
HOP = 64
highest = lax.Precision.HIGHEST


def passed_along(block, axis, distance):
    devices = range(lax.axis_size(axis))
    route = [(i - distance, i) for i in devices if i - distance in devices]
    return lax.ppermute(block, axis, route)


def spectral_table(length, start_column, width, weights):
    position = jnp.arange(length, dtype=jnp.int32)
    column = start_column + jnp.arange(width, dtype=jnp.int32)
    turns = position[:, None] * column[None, :] % length
    phase = turns.astype(jnp.float32) * (2.0 * math.pi / length)
    cosine = weights[:, None] * jnp.cos(phase)
    sinus = weights[:, None] * jnp.sin(phase)
    upper = jnp.stack([cosine, -sinus], axis=1)
    bottom = jnp.stack([sinus, cosine], axis=1)
    return jnp.stack([upper, bottom], axis=0)


def hann_weights():
    position = jnp.arange(C, dtype=jnp.int32).astype(jnp.float32)
    return (0.5 - 0.5 * jnp.cos(position * (2.0 * math.pi / C))) / math.sqrt(3.0 * C / 8.0)


def framed(samples, amount):
    blocks = samples.reshape(2, amount + C // HOP - 1, HOP)
    return jnp.concatenate(
        [blocks[:, offset : offset + amount] for offset in range(C // HOP)], axis=2
    )


def downconvert(spectra, start_channel, start_frame):
    channel = start_channel + jnp.arange(spectra.shape[1], dtype=jnp.int32)
    moment = start_frame + jnp.arange(spectra.shape[2], dtype=jnp.int32)
    turns = (channel * HOP % C)[:, None] * (moment % C)[None, :] % C
    phase = turns.astype(jnp.float32) * (2.0 * math.pi / C)
    cosine = jnp.cos(phase)
    sinus = jnp.sin(phase)
    real_part = spectra[0] * cosine + spectra[1] * sinus
    imag_part = spectra[1] * cosine - spectra[0] * sinus
    return jnp.stack([real_part, imag_part])


def channelize(frames, start_channel, width, start_frame):
    weights = spectral_table(C, start_channel, width, hann_weights())
    spectra = lax.dot_general(
        weights,
        frames,
        (((0, 1), (0, 2)), ((), ())),
        precision=highest,
        preferred_element_type=jnp.float32,
    )
    return downconvert(spectra, start_channel, start_frame)


def correlate(leading, trailing):
    lead_count = leading.shape[1]
    trail_count = trailing.shape[1]
    windows = leading.shape[2] // P_SIZE
    lead = leading.reshape(2, lead_count, windows, P_SIZE)
    trail = trailing.reshape(2, trail_count, windows, P_SIZE)
    real_part = lead[0][:, None] * trail[0][None] + lead[1][:, None] * trail[1][None]
    imag_part = lead[1][:, None] * trail[0][None] - lead[0][:, None] * trail[1][None]
    weights = spectral_table(
        P_SIZE, 0, P_SIZE, jnp.full((P_SIZE,), 1.0 / math.sqrt(P_SIZE), jnp.float32)
    )
    real_table = weights[0].reshape(P_SIZE, 2 * P_SIZE)
    imag_table = weights[1].reshape(P_SIZE, 2 * P_SIZE)
    dims = (((3,), (0,)), ((), ()))
    result = lax.dot_general(
        real_part, real_table, dims, precision=highest, preferred_element_type=jnp.float32
    )
    result = result + lax.dot_general(
        imag_part, imag_table, dims, precision=highest, preferred_element_type=jnp.float32
    )
    return result.reshape(lead_count, trail_count, windows, 2, P_SIZE)


def local(record):
    row_count = lax.axis_size("row")
    col_count = lax.axis_size("col")
    lead_width = C // row_count
    trail_width = C // col_count
    own_frames = record.shape[1] // HOP
    device = lax.axis_index("row") * col_count + lax.axis_index("col")
    follow = passed_along(record[:, : C - HOP], ("row", "col"), -1)
    frames = framed(jnp.concatenate([record, follow], axis=1), own_frames)
    spectra = channelize(frames, 0, C, device * own_frames)
    shaped = spectra.reshape(2, C, 1, 1, own_frames)
    leading = lax.all_to_all(shaped, "row", split_axis=1, concat_axis=2, tiled=True)
    leading = lax.all_gather(leading, "col", axis=3, tiled=True)
    trailing = lax.all_to_all(shaped, "col", split_axis=1, concat_axis=3, tiled=True)
    trailing = lax.all_gather(trailing, "row", axis=2, tiled=True)
    leading = leading.reshape(2, lead_width, -1)
    trailing = trailing.reshape(2, trail_width, -1)
    return correlate(leading, trailing)


def solution(mesh):
    return jax.shard_map(
        local,
        mesh=mesh,
        in_specs=(P(None, ("row", "col")),),
        out_specs=P("row", "col", None, None, None),
        check_vma=False,
    )
```

profile of v0, /device:TPU:0, one launch (start us, length us, event | category | flops | bytes accessed | tf_op | source)
XLA Modules:
  0.0 90.0 jit_solution(8008926294532363169)
XLA Ops:
  0.0 0.7 slice.43
  0.7 1.3 %collective-permute-start = (f32[2,192]{1,0:T(2,128)S(1)}, f32[2,192]{1,0:T(2,128)S(1)}, u32[]{:S(2)}, u32[]{:S(2)}) collective-permute-start(f32[2,192]{1,0:T(2,128)S(1)} %slice.43), channel_id=1, source_target_pairs={{1,0},{2,1},{3,2},{4,3},{5,4},{6,5},{7,6},{8,7},{9,8},{10,9},{11,1... | collective-permute-start | bytes 4616 | tf_op jit(solution)/shard_map/ppermute | solution.py:16
  2.0 1.0 %fusion.32 = f32[256,1,256]{2,0,1:T(8,128)S(1)} fusion(), kind=kLoop, calls=%fused_computation.40 | loop fusion | flops 1048576 | bytes 262144 | tf_op jit(solution)/shard_map/neg | solution.py:26
  3.0 1.1 %broadcast_multiply_fusion = (f32[256,1,256]{2,0,1:T(8,128)S(1)}, f32[256,1,256]{2,0,1:T(8,128)S(1)}) fusion(), kind=kLoop, calls=%fused_computation.34 | loop fusion | flops 1048576 | bytes 524288 | tf_op jit(solution)/shard_map/mul;broadcast_in_dim;broadcast_in_dim | solution.py:25
  4.1 1.1 %fusion.33 = (f32[256,1,256]{2,0,1:T(8,128)S(1)}, f32[256,1,256]{2,0,1:T(8,128)S(1)}, f32[256,1,256]{2,0,1:T(8,128)S(1)}) fusion(f32[256]{0:T(256)S(1)} %subtract_multiply_fusion), kind=kLoop, calls=%fused_computation.41 | loop fusion | flops 1114112 | bytes 787456 | tf_op jit(solution)/shard_map/neg | solution.py:26
  5.2 0.1 maximum_bitcast_fusion
  5.3 1.9 %collective-permute-done = f32[2,192]{1,0:T(2,128)S(1)} collective-permute-done((f32[2,192]{1,0:T(2,128)S(1)}, f32[2,192]{1,0:T(2,128)S(1)}, u32[]{:S(2)}, u32[]{:S(2)}) %collective-permute-start) | collective-permute-done | bytes 1568 | tf_op jit(solution)/shard_map/ppermute | solution.py:16
  7.2 0.7 pad_maximum_fusion.2
  7.9 0.1 reshape.348
  8.0 0.7 convolution_bitcast_fusion
  8.7 0.2 multiply_add_fusion
  8.8 0.1 copy.17
  9.0 0.9 %reshape.367 = f32[8,1,1024]{2,1,0:T(1,128)} reshape(f32[256,1,1,2,16]{4,3,2,1,0:T(2,128)S(1)} %bitcast.38) | data formatting | bytes 65536
  9.9 7.2 %all-to-all-start = ((f32[8,1,1024]{2,1,0:T(1,128)}), f32[8,1,1024]{2,1,0:T(1,128)S(1)}, u32[]{:S(2)}, u32[]{:S(2)}) async-start(f32[8,1,1024]{2,1,0:T(1,128)} %reshape.367), calls=%async_computation | async-start | bytes 65536 | tf_op jit(solution)/shard_map/all_to_all | solution.py:101
  17.2 0.1 pad_maximum_fusion
  17.2 0.2 copy.25
  17.4 0.2 copy.27
  17.7 0.9 %reshape.365 = f32[4,1,2048]{2,1,0:T(1,128)} reshape(f32[256,1,1,2,16]{4,3,2,1,0:T(2,128)S(1)} %bitcast.39) | data formatting | bytes 65536
  18.6 3.4 %all-to-all-done = f32[8,1,1024]{2,1,0:T(1,128)S(1)} async-done(((f32[8,1,1024]{2,1,0:T(1,128)}), f32[8,1,1024]{2,1,0:T(1,128)S(1)}, u32[]{:S(2)}, u32[]{:S(2)}) %all-to-all-start) | async-done | bytes 32800 | tf_op jit(solution)/shard_map/all_to_all | solution.py:101
  22.0 3.3 %all-to-all-start.1 = ((f32[4,1,2048]{2,1,0:T(1,128)}), f32[4,1,2048]{2,1,0:T(1,128)S(1)}, u32[]{:S(2)}, u32[]{:S(2)}) async-start(f32[4,1,2048]{2,1,0:T(1,128)} %reshape.365), calls=%async_computation.1 | async-start | bytes 65536 | tf_op jit(solution)/shard_map/all_to_all | solution.py:103
  25.3 0.5 broadcast.533
  25.8 0.6 reduce.1
  26.4 0.4 reshape.368
  26.8 0.1 copy.18
  27.0 15.8 %all-gather = f32[2,32,8,4,1,16]{1,5,3,2,4,0:T(8,128)S(1)} all-gather(f32[2,32,8,1,1,16]{1,5,3,2,4,0:T(8,128)S(1)} %bitcast.48), channel_id=2, replica_groups=mesh['row'=8,'col'=4] {'col'}, dimensions={3}, use_global_device_ids=true | all-gather | bytes 163840 | tf_op jit(solution)/shard_map/all_gather | solution.py:102
  42.8 0.1 copy.19
  42.9 0.1 copy.23
  43.0 0.0 all-to-all-done.1
  43.0 0.6 reduce
  43.7 0.4 reshape.366
  44.1 0.1 copy.21
  44.2 9.2 %all-gather.1 = f32[2,64,8,4,1,16]{1,5,3,2,4,0:T(8,128)S(1)} all-gather(f32[2,64,1,4,1,16]{1,5,3,2,4,0:T(8,128)S(1)} %bitcast.49), channel_id=3, replica_groups=mesh['row'=8,'col'=4] {'row'}, dimensions={2}, use_global_device_ids=true | all-gather | bytes 294912 | tf_op jit(solution)/shard_map/all_gather | solution.py:104
  53.5 0.1 copy.22
  53.6 0.1 copy.24
  53.7 7.9 %fusion = f32[32,64,2,512]{3,1,2,0:T(8,128)S(1)} fusion(f32[256,512,1,1]{0,1,3,2:T(8,128)S(1)} %bitcast.41, f32[64,2,256]{2,0,1:T(8,128)S(1)} %copy.24, f32[32,2,256]{2,1,0:T(2,128)S(1)} %copy.23, f32[64,2,256]{2,0,1:T(8,128)S(1)} %copy.22, f32[32,2,256]{2,1,0:T(2,128)S(1)} %copy.19), kind=kOutput, calls=%fused_computation | convolution fusion | flops 6445596672 | bytes 9306112 | tf_op jit(solution)/shard_map/dot_general | solution.py:84
  61.6 9.8 %fusion.8 = f32[32,64,2,512]{3,1,2,0:T(8,128)} fusion(f32[32,64,2,512]{3,1,2,0:T(8,128)S(1)} %fusion, f32[256,512,1,1]{0,1,3,2:T(8,128)S(1)} %bitcast.40, f32[64,2,256]{2,0,1:T(8,128)S(1)} %copy.24, f32[32,2,256]{2,1,0:T(2,128)S(1)} %copy.23, f32[64,2,256]{2,0,1:T(8,128)S(1)} %copy.22, f32[32,2,256]{2,1,0:T(2,128)S(1)} %copy.19), kind=kOutput, calls=%fused_computation.8 | convolution fusion | flops 6447693824 | bytes 17694720 | tf_op jit(solution)/shard_map/dot_general | solution.py:81
  71.4 10.6 %reshape.350 = f32[32,64,2,2,256]{4,3,1,2,0:T(2,128)} reshape(f32[32,64,2,512]{3,1,2,0:T(8,128)} %fusion.8) | data formatting | bytes 16777216 | tf_op jit(solution)/shard_map/reshape | solution.py:87
  81.9 8.0 %copy.29 = f32[32,64,2,2,256]{4,3,2,1,0:T(2,128)} copy(f32[32,64,2,2,256]{4,3,1,2,0:T(2,128)} %reshape.350) | data formatting | bytes 16777216 | tf_op jit(solution)/shard_map/reshape | solution.py:87
  (7 shorter events, 0.2 us)
Async XLA Ops:
  0.7 6.5 %collective-permute-start = (f32[2,192]{1,0:T(2,128)S(1)}, f32[2,192]{1,0:T(2,128)S(1)}, u32[]{:S(2)}, u32[]{:S(2)}) collective-permute-start(f32[2,192]{1,0:T(2,128)S(1)} %slice.43), channel_id=1, source_target_pairs={{1,0},{2,1},{3,2},{4,3},{5,4},{6,5},{7,6},{8,7},{9,8},{10,9},{11,1... | collective-permute-start | bytes 4616 | tf_op jit(solution)/shard_map/ppermute | solution.py:16
  9.9 12.1 %all-to-all-start = ((f32[8,1,1024]{2,1,0:T(1,128)}), f32[8,1,1024]{2,1,0:T(1,128)S(1)}, u32[]{:S(2)}, u32[]{:S(2)}) async-start(f32[8,1,1024]{2,1,0:T(1,128)} %reshape.367), calls=%async_computation | async-start | bytes 65536 | tf_op jit(solution)/shard_map/all_to_all | solution.py:101
  22.0 21.0 %all-to-all-start.1 = ((f32[4,1,2048]{2,1,0:T(1,128)}), f32[4,1,2048]{2,1,0:T(1,128)S(1)}, u32[]{:S(2)}, u32[]{:S(2)}) async-start(f32[4,1,2048]{2,1,0:T(1,128)} %reshape.365), calls=%async_computation.1 | async-start | bytes 65536 | tf_op jit(solution)/shard_map/all_to_all | solution.py:103
where the time goes:
time: 90.7 us; the launch traced here: 90 us
  blocking collectives  25 us (28%)
  local copies, waits for them, and re-layouts  23.8 us (26%)
  matrix products  18.3 us (20%)
  starting transfers between devices  11.8 us (13%)
  other arithmetic  5.47 us (6%)
  waiting for transfers between devices  5.31 us (6%)
    reshape x2, local copies, waits for them, and re-layouts, correlate(): return result.reshape(lead_count, trail_count, windows, 2, P_SIZE)  18.6 us
    all_gather x1, blocking collectives, local(): leading = lax.all_gather(leading, 'col', axis=3, tiled=True)  15.8 us
    dot_general x1, matrix products, correlate(): lax.dot_general(real_part, real_table, dims, precision=highest, preferred...  9.76 us
    all_gather x1, blocking collectives, local(): trailing = lax.all_gather(trailing, 'row', axis=2, tiled=True)  9.23 us
    dot_general x1, matrix products, correlate(): lax.dot_general(imag_part, imag_table, dims, precision=highest, preferred...  7.91 us
    all_to_all x1, starting transfers between devices, local(): lax.all_to_all(shaped, 'row', split_axis=1, concat_axis=2, tiled=True)  7.24 us
    all_to_all x1, waiting for transfers between devices, local(): lax.all_to_all(shaped, 'row', split_axis=1, concat_axis=2, tiled=True)  3.4 us
    all_to_all x1, starting transfers between devices, local(): lax.all_to_all(shaped, 'col', split_axis=1, concat_axis=3, tiled=True)  3.3 us
  transfers between devices with their start and end apart: 3, of which 2 were waited for; matrix products, arithmetic and copies ran while one was open for 7% of the time, Pallas kernels for 0%

commit v1 on v0

--- a/solution.py
+++ b/solution.py
@@ -101,7 +101,12 @@
     leading = lax.all_to_all(shaped, "row", split_axis=1, concat_axis=2, tiled=True)
     leading = lax.all_gather(leading, "col", axis=3, tiled=True)
     trailing = lax.all_to_all(shaped, "col", split_axis=1, concat_axis=3, tiled=True)
-    trailing = lax.all_gather(trailing, "row", axis=2, tiled=True)
+    ring = [trailing]
+    for hop in range(7):
+        ring.append(lax.ppermute(ring[-1], "row", [(dev, (dev + 1) % 8) for dev in range(8)]))
+    trailing = jnp.roll(
+        jnp.concatenate(ring[::-1], axis=2), (lax.axis_index("row") + 1) * ring[0].shape[2], axis=2
+    )
     leading = leading.reshape(2, lead_width, -1)
     trailing = trailing.reshape(2, trail_width, -1)
     return correlate(leading, trailing)

time: 90.7 us -> 107 us (1.18)
  waiting for transfers between devices: 5.31 us -> 24.9 us
  starting transfers between devices: 11.8 us -> 5.87 us
  blocking collectives: 25 us -> 28.2 us
    ppermute x0 -> x7, waiting for transfers between devices: none -> 17 us  [local(): lax.ppermute(ring[-1], 'row', [(dev, (dev + 1) % 8) for dev in range(8)])]
    all_to_all x0 -> x1, blocking collectives: none -> 12 us  [local(): lax.all_to_all(shaped, 'col', split_axis=1, concat_axis=3, tiled=True)]
    all_gather x1 -> x0, blocking collectives: 9.23 us -> none  [local(): trailing = lax.all_gather(trailing, 'row', axis=2, tiled=True)]
    all_to_all x1 -> x0, starting transfers between devices: 3.3 us -> none  [local(): lax.all_to_all(shaped, 'col', split_axis=1, concat_axis=3, tiled=True)]
    all_to_all x1, starting transfers between devices: 7.24 us -> 3.97 us  [local(): lax.all_to_all(shaped, 'row', split_axis=1, concat_axis=2, tiled=True)]
    ppermute x1, waiting for transfers between devices: 1.91 us -> 3.95 us  [passed_along(): return lax.ppermute(block, axis, route)]
    unnamed x4 -> x19, local copies, waits for them, and re-layouts: 2.65 us -> 2.15 us
  transfers between devices with their start and end apart: 3 -> 9, of which waited for: 2 -> 6; matrix products, arithmetic and copies ran while one was open for 7% -> 6% of each run, Pallas kernels for 0% -> 0%
where the time goes in v1:
time: 107 us
  blocking collectives  28.2 us (26%)
  waiting for transfers between devices  24.9 us (23%)
  local copies, waits for them, and re-layouts  23.4 us (22%)
  matrix products  18.3 us (17%)
  starting transfers between devices  5.87 us (5%)
  other arithmetic  5.62 us (5%)
    reshape x2, local copies, waits for them, and re-layouts, correlate(): return result.reshape(lead_count, trail_count, windows, 2, P_SIZE)  18.6 us
    ppermute x7, waiting for transfers between devices, local(): lax.ppermute(ring[-1], 'row', [(dev, (dev + 1) % 8) for dev in range(8)])  17 us
    all_gather x1, blocking collectives, local(): leading = lax.all_gather(leading, 'col', axis=3, tiled=True)  16.2 us
    all_to_all x1, blocking collectives, local(): lax.all_to_all(shaped, 'col', split_axis=1, concat_axis=3, tiled=True)  12 us
    dot_general x1, matrix products, correlate(): lax.dot_general(real_part, real_table, dims, precision=highest, preferred...  9.75 us
    dot_general x1, matrix products, correlate(): lax.dot_general(imag_part, imag_table, dims, precision=highest, preferred...  7.91 us
    all_to_all x1, waiting for transfers between devices, local(): lax.all_to_all(shaped, 'row', split_axis=1, concat_axis=2, tiled=True)  3.99 us
    all_to_all x1, starting transfers between devices, local(): lax.all_to_all(shaped, 'row', split_axis=1, concat_axis=2, tiled=True)  3.97 us
  transfers between devices with their start and end apart: 9, of which 6 were waited for; matrix products, arithmetic and copies ran while one was open for 6% of the time, Pallas kernels for 0%

profile of v1, /device:TPU:0, one launch (start us, length us, event | category | flops | bytes accessed | tf_op | source)
XLA Modules:
  0.0 106.8 jit_solution(7558239780874186439)
XLA Ops:
  0.0 0.7 slice.43
  0.7 1.3 %collective-permute-start = (f32[2,192]{1,0:T(2,128)S(1)}, f32[2,192]{1,0:T(2,128)S(1)}, u32[]{:S(2)}, u32[]{:S(2)}) collective-permute-start(f32[2,192]{1,0:T(2,128)S(1)} %slice.43), channel_id=1, source_target_pairs={{1,0},{2,1},{3,2},{4,3},{5,4},{6,5},{7,6},{8,7},{9,8},{10,9},{11,1... | collective-permute-start | bytes 4616 | tf_op jit(solution)/shard_map/ppermute | solution.py:16
  2.0 1.1 %fusion.33 = (f32[256,1,256]{2,0,1:T(8,128)S(1)}, f32[256,1,256]{2,0,1:T(8,128)S(1)}, f32[256,1,256]{2,0,1:T(8,128)S(1)}) fusion(f32[256]{0:T(256)S(1)} %subtract_multiply_fusion), kind=kLoop, calls=%fused_computation.41 | loop fusion | flops 1114112 | bytes 787456 | tf_op jit(solution)/shard_map/neg | solution.py:26
  3.1 0.1 maximum_bitcast_fusion
  3.2 4.0 %collective-permute-done = f32[2,192]{1,0:T(2,128)S(1)} collective-permute-done((f32[2,192]{1,0:T(2,128)S(1)}, f32[2,192]{1,0:T(2,128)S(1)}, u32[]{:S(2)}, u32[]{:S(2)}) %collective-permute-start) | collective-permute-done | bytes 1568 | tf_op jit(solution)/shard_map/ppermute | solution.py:16
  7.2 0.7 pad_maximum_fusion.2
  7.9 0.1 reshape.348
  8.0 0.7 convolution_bitcast_fusion
  8.7 0.2 multiply_add_fusion
  8.8 0.1 copy.17
  9.0 0.3 reshape.360
  9.3 12.0 %all_to_all.36 = f32[4,1,2048]{2,1,0:T(1,128)S(1)} all-to-all(f32[4,1,2048]{2,1,0:T(1,128)S(1)} %reshape.360), channel_id=1, replica_groups=mesh['row'=8,'col'=4] {'col'}, dimensions={0} | all-to-all | bytes 65536 | tf_op jit(solution)/shard_map/all_to_all | solution.py:103
  21.3 0.5 broadcast.534
  21.8 0.7 reduce
  22.6 0.4 reshape.361
  22.9 0.1 copy.21
  23.1 0.0 collective-permute-start.1
  23.1 4.6 %collective-permute-done.1 = f32[2,64,1,4,16]{1,4,3,2,0:T(8,128)S(1)} collective-permute-done((f32[2,64,1,4,16]{1,4,3,2,0:T(8,128)S(1)}, f32[2,64,1,4,16]{1,4,3,2,0:T(8,128)S(1)}, u32[]{:S(2)}, u32[]{:S(2)}) %collective-permute-start.1) | collective-permute-done | bytes 32800 | tf_op jit(solution)/shard_map/ppermute | solution.py:106
  27.7 0.0 collective-permute-start.2
  27.7 4.6 %collective-permute-done.2 = f32[2,64,1,4,16]{1,4,3,2,0:T(8,128)S(1)} collective-permute-done((f32[2,64,1,4,16]{1,4,3,2,0:T(8,128)S(1)}, f32[2,64,1,4,16]{1,4,3,2,0:T(8,128)S(1)}, u32[]{:S(2)}, u32[]{:S(2)}) %collective-permute-start.2) | collective-permute-done | bytes 32800 | tf_op jit(solution)/shard_map/ppermute | solution.py:106
  32.3 0.0 collective-permute-start.3
  32.3 1.1 broadcast_multiply_fusion
  33.4 3.5 %collective-permute-done.3 = f32[2,64,1,4,16]{1,4,3,2,0:T(8,128)S(1)} collective-permute-done((f32[2,64,1,4,16]{1,4,3,2,0:T(8,128)S(1)}, f32[2,64,1,4,16]{1,4,3,2,0:T(8,128)S(1)}, u32[]{:S(2)}, u32[]{:S(2)}) %collective-permute-start.3) | collective-permute-done | bytes 32800 | tf_op jit(solution)/shard_map/ppermute | solution.py:106
  36.9 0.0 collective-permute-start.4
  36.9 1.0 fusion.32
  37.9 1.0 reshape.362
  38.8 4.0 %all-to-all-start = ((f32[8,1,1024]{2,1,0:T(1,128)}), f32[8,1,1024]{2,1,0:T(1,128)S(1)}, u32[]{:S(2)}, u32[]{:S(2)}) async-start(f32[8,1,1024]{2,1,0:T(1,128)} %reshape.362), calls=%async_computation | async-start | bytes 65536 | tf_op jit(solution)/shard_map/all_to_all | solution.py:101
  42.8 0.0 collective-permute-done.4
  42.8 0.5 collective-permute-start.5
  43.3 0.1 pad_maximum_fusion
  43.4 0.2 copy.25
  43.6 0.2 copy.27
  43.8 4.0 %all-to-all-done = f32[8,1,1024]{2,1,0:T(1,128)S(1)} async-done(((f32[8,1,1024]{2,1,0:T(1,128)}), f32[8,1,1024]{2,1,0:T(1,128)S(1)}, u32[]{:S(2)}, u32[]{:S(2)}) %all-to-all-start) | async-done | bytes 32800 | tf_op jit(solution)/shard_map/all_to_all | solution.py:101
  47.8 0.7 reduce.1
  48.5 0.4 reshape.363
  48.9 0.1 copy.18
  49.1 0.0 collective-permute-done.5
  49.1 0.1 collective-permute-start.6
  49.1 16.2 %all-gather = f32[2,32,8,4,1,16]{1,5,3,2,4,0:T(8,128)S(1)} all-gather(f32[2,32,8,1,1,16]{1,5,3,2,4,0:T(8,128)S(1)} %bitcast.53), channel_id=2, replica_groups=mesh['row'=8,'col'=4] {'col'}, dimensions={3}, use_global_device_ids=true | all-gather | bytes 163840 | tf_op jit(solution)/shard_map/all_gather | solution.py:102
  65.4 0.0 collective-permute-done.6
  65.4 0.0 collective-permute-start.7
  65.4 0.1 copy.19
  65.5 0.1 copy.23
  65.7 4.3 %collective-permute-done.7 = f32[2,64,1,4,16]{1,4,3,2,0:T(8,128)S(1)} collective-permute-done((f32[2,64,1,4,16]{1,4,3,2,0:T(8,128)S(1)}, f32[2,64,1,4,16]{1,4,3,2,0:T(8,128)S(1)}, u32[]{:S(2)}, u32[]{:S(2)}) %collective-permute-start.7) | collective-permute-done | bytes 32800 | tf_op jit(solution)/shard_map/ppermute | solution.py:106
  70.3 0.1 copy.22
  70.4 0.1 copy.24
  70.5 7.9 %fusion = f32[32,64,2,512]{3,1,2,0:T(8,128)S(1)} fusion(f32[256,512,1,1]{0,1,3,2:T(8,128)S(1)} %bitcast.45, f32[64,2,256]{2,0,1:T(8,128)S(1)} %copy.24, f32[32,2,256]{2,1,0:T(2,128)S(1)} %copy.23, f32[64,2,256]{2,0,1:T(8,128)S(1)} %copy.22, f32[32,2,256]{2,1,0:T(2,128)S(1)} %copy.19), kind=kOutput, calls=%fused_computation | convolution fusion | flops 6445596672 | bytes 9306112 | tf_op jit(solution)/shard_map/dot_general | solution.py:84
  78.4 9.8 %fusion.8 = f32[32,64,2,512]{3,1,2,0:T(8,128)} fusion(f32[32,64,2,512]{3,1,2,0:T(8,128)S(1)} %fusion, f32[256,512,1,1]{0,1,3,2:T(8,128)S(1)} %bitcast.44, f32[64,2,256]{2,0,1:T(8,128)S(1)} %copy.24, f32[32,2,256]{2,1,0:T(2,128)S(1)} %copy.23, f32[64,2,256]{2,0,1:T(8,128)S(1)} %copy.22, f32[32,2,256]{2,1,0:T(2,128)S(1)} %copy.19), kind=kOutput, calls=%fused_computation.8 | convolution fusion | flops 6447693824 | bytes 17694720 | tf_op jit(solution)/shard_map/dot_general | solution.py:81
  88.2 10.6 %reshape.350 = f32[32,64,2,2,256]{4,3,1,2,0:T(2,128)} reshape(f32[32,64,2,512]{3,1,2,0:T(8,128)} %fusion.8) | data formatting | bytes 16777216 | tf_op jit(solution)/shard_map/reshape | solution.py:87
  98.7 8.0 %copy.29 = f32[32,64,2,2,256]{4,3,2,1,0:T(2,128)} copy(f32[32,64,2,2,256]{4,3,1,2,0:T(2,128)} %reshape.350) | data formatting | bytes 16777216 | tf_op jit(solution)/shard_map/reshape | solution.py:87
  (23 shorter events, 0.3 us)
Async XLA Ops:
  0.7 6.5 %collective-permute-start = (f32[2,192]{1,0:T(2,128)S(1)}, f32[2,192]{1,0:T(2,128)S(1)}, u32[]{:S(2)}, u32[]{:S(2)}) collective-permute-start(f32[2,192]{1,0:T(2,128)S(1)} %slice.43), channel_id=1, source_target_pairs={{1,0},{2,1},{3,2},{4,3},{5,4},{6,5},{7,6},{8,7},{9,8},{10,9},{11,1... | collective-permute-start | bytes 4616 | tf_op jit(solution)/shard_map/ppermute | solution.py:16
  23.1 4.6 %collective-permute-start.1 = (f32[2,64,1,4,16]{1,4,3,2,0:T(8,128)S(1)}, f32[2,64,1,4,16]{1,4,3,2,0:T(8,128)S(1)}, u32[]{:S(2)}, u32[]{:S(2)}) collective-permute-start(f32[2,64,1,4,16]{1,4,3,2,0:T(8,128)S(1)} %bitcast.52), channel_id=1, source_target_pairs={{0,4},{4,8},{8,12},{12,16},{16,20},{20,24},{24,28},{28,0},{1,5},{5... | collective-permute-start | bytes 98312 | tf_op jit(solution)/shard_map/ppermute | solution.py:106
  27.7 4.6 %collective-permute-start.2 = (f32[2,64,1,4,16]{1,4,3,2,0:T(8,128)S(1)}, f32[2,64,1,4,16]{1,4,3,2,0:T(8,128)S(1)}, u32[]{:S(2)}, u32[]{:S(2)}) collective-permute-start(f32[2,64,1,4,16]{1,4,3,2,0:T(8,128)S(1)} %collective-permute-done.1), channel_id=1, source_target_pairs={{0,4},{4,8},{8,12},{12,16},{16,20},{20,24},{24,28},{28,0},{1,5},{5... | collective-permute-start | bytes 98312 | tf_op jit(solution)/shard_map/ppermute | solution.py:106
  32.3 4.6 %collective-permute-start.3 = (f32[2,64,1,4,16]{1,4,3,2,0:T(8,128)S(1)}, f32[2,64,1,4,16]{1,4,3,2,0:T(8,128)S(1)}, u32[]{:S(2)}, u32[]{:S(2)}) collective-permute-start(f32[2,64,1,4,16]{1,4,3,2,0:T(8,128)S(1)} %collective-permute-done.2), channel_id=1, source_target_pairs={{0,4},{4,8},{8,12},{12,16},{16,20},{20,24},{24,28},{28,0},{1,5},{5... | collective-permute-start | bytes 98312 | tf_op jit(solution)/shard_map/ppermute | solution.py:106
  36.9 5.9 %collective-permute-start.4 = (f32[2,64,1,4,16]{1,4,3,2,0:T(8,128)S(1)}, f32[2,64,1,4,16]{1,4,3,2,0:T(8,128)S(1)}, u32[]{:S(2)}, u32[]{:S(2)}) collective-permute-start(f32[2,64,1,4,16]{1,4,3,2,0:T(8,128)S(1)} %collective-permute-done.3), channel_id=1, source_target_pairs={{0,4},{4,8},{8,12},{12,16},{16,20},{20,24},{24,28},{28,0},{1,5},{5... | collective-permute-start | bytes 98312 | tf_op jit(solution)/shard_map/ppermute | solution.py:106
  38.8 9.0 %all-to-all-start = ((f32[8,1,1024]{2,1,0:T(1,128)}), f32[8,1,1024]{2,1,0:T(1,128)S(1)}, u32[]{:S(2)}, u32[]{:S(2)}) async-start(f32[8,1,1024]{2,1,0:T(1,128)} %reshape.362), calls=%async_computation | async-start | bytes 65536 | tf_op jit(solution)/shard_map/all_to_all | solution.py:101
  42.8 6.3 %collective-permute-start.5 = (f32[2,64,1,4,16]{1,4,3,2,0:T(8,128)S(1)}, f32[2,64,1,4,16]{1,4,3,2,0:T(8,128)S(1)}, u32[]{:S(2)}, u32[]{:S(2)}) collective-permute-start(f32[2,64,1,4,16]{1,4,3,2,0:T(8,128)S(1)} %collective-permute-done.4), channel_id=1, source_target_pairs={{0,4},{4,8},{8,12},{12,16},{16,20},{20,24},{24,28},{28,0},{1,5},{5... | collective-permute-start | bytes 98312 | tf_op jit(solution)/shard_map/ppermute | solution.py:106
  49.1 16.3 %collective-permute-start.6 = (f32[2,64,1,4,16]{1,4,3,2,0:T(8,128)S(1)}, f32[2,64,1,4,16]{1,4,3,2,0:T(8,128)S(1)}, u32[]{:S(2)}, u32[]{:S(2)}) collective-permute-start(f32[2,64,1,4,16]{1,4,3,2,0:T(8,128)S(1)} %collective-permute-done.5), channel_id=1, source_target_pairs={{0,4},{4,8},{8,12},{12,16},{16,20},{20,24},{24,28},{28,0},{1,5},{5... | collective-permute-start | bytes 98312 | tf_op jit(solution)/shard_map/ppermute | solution.py:106
  65.4 4.6 %collective-permute-start.7 = (f32[2,64,1,4,16]{1,4,3,2,0:T(8,128)S(1)}, f32[2,64,1,4,16]{1,4,3,2,0:T(8,128)S(1)}, u32[]{:S(2)}, u32[]{:S(2)}) collective-permute-start(f32[2,64,1,4,16]{1,4,3,2,0:T(8,128)S(1)} %collective-permute-done.6), channel_id=1, source_target_pairs={{0,4},{4,8},{8,12},{12,16},{16,20},{20,24},{24,28},{28,0},{1,5},{5... | collective-permute-start | bytes 98312 | tf_op jit(solution)/shard_map/ppermute | solution.py:106
